TPU v7x, 32 devices: a whole 2x2x4 slice. The times are simulated.
32 devices in a mesh: groups: 2 (over y), expert: 4 (over z), dp: 2 (over core), tensor: 2 (over x).
Axes of the slice: x: 2, y: 2, z: 4, core: 2. Of those that a mesh axis runs over, the one named last changes fastest.
Arguments:
- tokens: bfloat16 [2, 2048, 2048], P('dp', ('groups', 'expert', 'tensor')), parts along dimension 1, may hold values from -6 to 6
- proj_weight: bfloat16 [4, 2048, 3584], P('expert', 'dp', 'tensor'), may hold values from -0.125 to 0.125
- slot_grads: bfloat16 [2, 4, 32, 3584], P('dp', 'expert', 'groups', 'tensor'), parts along dimension 2, may hold values from -1.5 to 1.5
- gate_weights: float32 [2, 2, 32], P('dp', None, 'groups'), parts along dimension 2, may hold values from 0.2 to 1
- selected: int32 [2, 2, 32], P('dp', None, 'groups'), parts along dimension 2, may hold values from 0 to 1023, as said below
Outputs:
- token_grads: bfloat16 [2, 2048, 2048], P('dp', ('groups', 'expert', 'tensor')), parts along dimension 1
- weight_grads: bfloat16 [8, 2048, 3584], P(('groups', 'expert'), 'dp', 'tensor'), parts along dimension 0
There are 2 independent parts, one for each index of `groups`. A program takes and returns all parts, laid end to end along the dimension named above; an argument that names none is the same for every part. Nothing has to cross between parts.
Inputs may be any that keep to these rules, and one draw needn't show every extreme that they name: `selected`: each entry names a token of its own group. Within one group and one expert the 16 entries are distinct. In each group an expert takes at most 4 tokens from the 128 tokens of one device (tokens k * 128 to (k + 1) * 128 - 1), and exactly 4 from some devices.
All inputs are finite; a program needn't handle non-finite values.
Results may differ from a plain program's by a relative error of at most 0.011.
Values may be sent and summed in bfloat16 or wider, within the bound.
No kernel may reach another device: no remote copies, remote signals or barrier semaphores. Data moves between devices by JAX's collectives and lax.ppermute only.
A program may use at most 64 MiB of HBM per device.

v0:
```python
import jax
import jax.numpy as jnp
from jax import lax
from jax.sharding import PartitionSpec as P

MOST = 4


def local(tokens, proj_weight, slot_grads, gate_weights, selected):
    n_tensor = lax.axis_size("tensor")
    n_expert = lax.axis_size("expert")
    n_data = lax.axis_size("dp")
    owners = n_expert * n_tensor
    own_expert = lax.axis_index("expert")
    own_owner = own_expert * n_tensor + lax.axis_index("tensor")
    token_rows = tokens[0]
    tok_dev = token_rows.shape[0]
    features = token_rows.shape[1]
    chosen = selected[0]
    experts = chosen.shape[0]
    capacity = chosen.shape[1]
    owner_of = chosen // tok_dev
    local_row = chosen % tok_dev
    slot_ids = jnp.arange(capacity)
    earlier = slot_ids[None, :] < slot_ids[:, None]
    same_owner = owner_of[:, :, None] == owner_of[:, None, :]
    arrival = jnp.sum(same_owner & earlier[None], axis=2)
    slot_pos = jnp.arange(MOST)
    local_hits = owner_of == own_owner
    selector = local_hits[:, None, :] & (arrival[:, None, :] == slot_pos[None, :, None])
    filled = jnp.any(selector, axis=2)
    send_row = jnp.sum(jnp.where(selector, local_row[:, None, :], 0), axis=2)
    outgoing = jnp.where(filled[..., None], token_rows[send_row], jnp.zeros((), jnp.bfloat16))
    outgoing_all = jnp.broadcast_to(outgoing[:, None, None], (experts, 2, n_tensor, MOST, features))
    incoming = lax.all_to_all(
        outgoing_all.reshape(owners, MOST, features),
        ("expert", "tensor"),
        split_axis=0,
        concat_axis=0,
        tiled=True,
    )
    incoming = incoming.reshape(owners * MOST, features)
    own_index = own_expert // 2
    own_owners = lax.dynamic_index_in_dim(owner_of, own_index, 0, keepdims=False)
    own_arrival = lax.dynamic_index_in_dim(arrival, own_index, 0, keepdims=False)
    slot_rows = incoming[own_owners * MOST + own_arrival]
    gate_row = lax.dynamic_index_in_dim(gate_weights[0], own_index, 0, keepdims=False)
    scaled = (gate_row[:, None] * slot_grads[0, 0].astype(jnp.float32)).astype(jnp.bfloat16)
    partial_value_sum = lax.dot_general(
        scaled,
        lax.all_gather(proj_weight, "dp", axis=1, tiled=True)[0],
        (((1,), (1,)), ((), ())),
        preferred_element_type=jnp.float32,
    ).astype(jnp.bfloat16)
    slot_equal_mask = (own_owners[None, None, :] == jnp.arange(owners)[:, None, None]) & (
        own_arrival[None, None, :] == slot_pos[None, :, None]
    )
    slot_used = jnp.any(slot_equal_mask, axis=2)
    slot_index = jnp.sum(jnp.where(slot_equal_mask, slot_ids[None, None, :], 0), axis=2)
    returning = jnp.where(
        slot_used[..., None], partial_value_sum[slot_index], jnp.zeros((), jnp.bfloat16)
    )
    arrived = lax.all_to_all(
        returning, ("expert", "tensor"), split_axis=0, concat_axis=0, tiled=True
    )
    arrived = arrived.reshape(owners * MOST, features)
    complete_row = jnp.broadcast_to(send_row[:, None, None], (experts, 2, n_tensor, MOST)).reshape(
        owners * MOST
    )
    used_full = jnp.broadcast_to(filled[:, None, None], (experts, 2, n_tensor, MOST)).reshape(
        owners * MOST
    )
    placement = (jnp.arange(tok_dev)[:, None] == complete_row[None, :]) & used_full[None, :]
    token_grads = jnp.dot(
        placement.astype(jnp.bfloat16), arrived, preferred_element_type=jnp.float32
    )
    token_grads = token_grads.astype(jnp.bfloat16)[None]
    column_share = lax.all_to_all(slot_rows, "dp", split_axis=1, concat_axis=0, tiled=True)
    scaled_all = lax.all_gather(scaled, "dp", axis=0, tiled=True)
    column_share = column_share.reshape(n_data, capacity, column_share.shape[1])
    scaled_all = scaled_all.reshape(n_data, capacity, scaled_all.shape[1])
    per_group = jnp.einsum(
        "gcd,gcf->gdf", column_share, scaled_all, preferred_element_type=jnp.float32
    )
    per_group = per_group.astype(jnp.bfloat16).astype(jnp.float32)
    weight_grads = jnp.sum(per_group, axis=0).astype(jnp.bfloat16)[None]
    return (token_grads, weight_grads)


def solution(mesh):
    in_specs = (
        P("dp", ("groups", "expert", "tensor"), None),
        P("expert", "dp", "tensor"),
        P("dp", "expert", "groups", "tensor"),
        P("dp", None, "groups"),
        P("dp", None, "groups"),
    )
    out_specs = (
        P("dp", ("groups", "expert", "tensor"), None),
        P(("groups", "expert"), "dp", "tensor"),
    )
    return jax.shard_map(local, mesh=mesh, in_specs=in_specs, out_specs=out_specs, check_vma=False)
```

profile of v0, /device:TPU:0, one launch (start us, length us, event | category | flops | bytes accessed | tf_op | source)
XLA Modules:
  0.0 58.4 jit_solution(3440165395489555670)
XLA Ops:
  7.2 0.7 %all-gather.2.cloned.1.call-update = ((bf16[1,1024,1792]{2,1,0:T(8,128)(2,1)}), bf16[1,2048,1792]{2,1,0:T(8,128)(2,1)}) async-update(((), (), s32[]{:S(2)}) %all-gather.2.cloned.1.call-start, bf16[1,1024,1792]{2,1,0:T(8,128)(2,1)} %param.6) | async-update | bytes 14680088
  7.9 0.7 %broadcast_compare_fusion = (pred[2,16]{1,0:T(4,128)(4,1)S(1)}, s32[2,16]{1,0:T(2,128)S(1)}) fusion(s32[]{:T(128)S(6)} %add.79, s32[1,2,16]{2,1,0:T(2,128)} %param.9), kind=kLoop, calls=%fused_computation.53 | loop fusion | flops 512 | bytes 292 | tf_op jit(solution)/shard_map/eq | solution.py:29
  8.6 0.2 convert_reduce_fusion.1
  8.8 0.7 %and_select_fusion.1 = s32[2,16]{1,0:T(2,128)S(1)} fusion(s32[1,2,16]{2,1,0:T(2,128)} %param.9), kind=kLoop, calls=%fused_computation.41 | loop fusion | flops 352 | bytes 256 | tf_op jit(solution)/shard_map/jit(remainder)/select_n | solution.py:23
  9.5 0.1 select_reduce_fusion
  9.7 0.1 reshape.265
  9.8 0.6 gather_fusion.1
  10.4 0.2 fusion.19
  10.5 0.1 broadcast_select_fusion.1
  10.6 0.7 %broadcast_in_dim.104 = bf16[2,2,2,4,2048]{4,3,2,1,0:T(4,128)(2,1)} broadcast(bf16[2,4,2048]{2,1,0:T(4,128)(2,1)S(1)} %broadcast_select_fusion.1), dimensions={0,3,4} | broadcast | bytes 163840 | tf_op jit(solution)/shard_map/broadcast_in_dim | solution.py:34
  11.3 7.3 %all-to-all-start.1 = ((bf16[8,4,2048]{2,1,0:T(4,128)(2,1)}), bf16[8,4,2048]{2,1,0:T(4,128)(2,1)S(1)}, u32[]{:S(2)}, u32[]{:S(2)}) async-start(bf16[8,4,2048]{2,1,0:T(4,128)(2,1)} %bitcast.10), calls=%async_computation.1 | async-start | bytes 262144 | tf_op jit(solution)/shard_map/all_to_all | solution.py:35
  18.6 0.7 %fusion.20 = f32[16]{0:T(128)S(1)} fusion(f32[1,2,16]{2,1,0:T(2,128)} %param.8, s32[]{:T(128)S(6)} %select_n.92), kind=kLoop, calls=%fused_computation.51 | loop fusion | bytes 132 | tf_op jit(solution)/shard_map/jit(dynamic_index_in_dim)/dynamic_slice | solution.py:47
  19.3 0.2 and_reduce_fusion
  19.5 0.2 fusion.17
  19.6 0.9 %fusion.8 = bf16[16,1792]{1,0:T(8,128)(2,1)S(1)} fusion(bf16[1,1,16,1792]{3,2,1,0:T(8,128)(2,1)} %param.7, f32[16]{0:T(128)S(1)} %fusion.20), kind=kLoop, calls=%fused_computation.14 | loop fusion | flops 86016 | bytes 114752 | tf_op jit(solution)/shard_map/convert_element_type | solution.py:48
  20.5 0.1 copy.10
  20.6 0.1 copy.11
  20.7 0.1 reshape.257
  20.8 0.1 and.91
  20.9 0.1 eq.100
  21.0 4.9 %all-to-all-done.1 = bf16[8,4,2048]{2,1,0:T(4,128)(2,1)S(1)} async-done(((bf16[8,4,2048]{2,1,0:T(4,128)(2,1)}), bf16[8,4,2048]{2,1,0:T(4,128)(2,1)S(1)}, u32[]{:S(2)}, u32[]{:S(2)}) %all-to-all-start.1) | async-done | bytes 131104 | tf_op jit(solution)/shard_map/all_to_all | solution.py:35
  26.0 0.6 %gather_fusion.2 = bf16[16,2048]{1,0:T(8,128)(2,1)S(1)} fusion(bf16[32,2048]{1,0:T(8,128)(2,1)S(1)} %reshape.252, s32[1024]{0:T(1024)S(1)} %pad_clamp_fusion), kind=kCustom, calls=%fused_computation.2 | custom fusion | bytes 131136 | tf_op jit(solution)/shard_map/gather | solution.py:46
  26.6 0.6 %copy.15 = bf16[2,2,8,1024]{3,2,0,1:T(8,128)(2,1)} copy(bf16[2,2,8,1024]{3,2,1,0:T(8,128)(2,1)S(1)} %bitcast.71) | data formatting | bytes 131072 | tf_op jit(solution)/shard_map/all_to_all | solution.py:78
  27.2 3.3 %all-to-all-start.2 = ((bf16[16,2,1024]{2,0,1:T(8,128)(2,1)}), bf16[16,2,1024]{2,0,1:T(8,128)(2,1)S(1)}, u32[]{:S(2)}, u32[]{:S(2)}) async-start(bf16[16,2,1024]{2,0,1:T(8,128)(2,1)} %bitcast.67), calls=%async_computation.2 | async-start | bytes 131072 | tf_op jit(solution)/shard_map/all_to_all | solution.py:78
  30.6 5.1 %fusion.3 = bf16[16,2048]{1,0:T(8,128)(2,1)S(1)} fusion(bf16[1,2048,1792]{2,1,0:T(8,128)(2,1)} %all-gather.2.cloned.1.call-done, bf16[1,1,16,1792]{3,2,1,0:T(8,128)(2,1)} %param.7, f32[16]{0:T(128)S(1)} %fusion.20), kind=kOutput, calls=%fused_computation.8 | convolution fusion | flops 117559296 | bytes 7462976 | tf_op jit(solution)/shard_map/dot_general | solution.py:49
  35.7 0.7 %gather_fusion = bf16[32,2048]{1,0:T(8,128)(2,1)S(1)} fusion(bf16[16,2048]{1,0:T(8,128)(2,1)S(1)} %fusion.3, s32[1024]{0:T(1024)S(1)} %pad_clamp_fusion.2), kind=kCustom, calls=%fused_computation | custom fusion | bytes 262272 | tf_op jit(solution)/shard_map/gather | solution.py:61
  36.4 0.8 %broadcast_select_fusion = bf16[8,4,2048]{2,1,0:T(4,128)(2,1)} fusion(bf16[8,4,2048]{2,1,0:T(4,128)(2,1)S(1)} %reshape.256, pred[8,4]{1,0:T(8,128)(4,1)S(1)} %copy.10), kind=kLoop, calls=%fused_computation.11 | loop fusion | flops 65536 | bytes 262176 | tf_op jit(solution)/shard_map/jit(_where)/select_n | solution.py:60
  37.2 5.8 %all-to-all-start = ((bf16[8,4,2048]{2,1,0:T(4,128)(2,1)}), bf16[8,4,2048]{2,1,0:T(4,128)(2,1)S(1)}, u32[]{:S(2)}, u32[]{:S(2)}) async-start(bf16[8,4,2048]{2,1,0:T(4,128)(2,1)} %broadcast_select_fusion), calls=%async_computation | async-start | bytes 262144 | tf_op jit(solution)/shard_map/all_to_all | solution.py:63
  43.0 1.9 %all_gather.7 = bf16[32,1792]{1,0:T(8,128)(2,1)S(1)} all-gather(bf16[16,1792]{1,0:T(8,128)(2,1)S(1)} %fusion.8), channel_id=1, replica_groups=mesh['groups'=2,'expert'=4,'dp'=2,'tensor'=2] {'dp'}, dimensions={0}, use_global_device_ids=true | all-gather | bytes 172032 | tf_op jit(solution)/shard_map/all_gather | solution.py:79
  44.9 4.3 %convert_reduce_fusion = bf16[1024,1792]{1,0:T(8,128)(2,1)} fusion(bf16[2,16,1792]{2,1,0:T(8,128)(2,1)S(1)} %bitcast.70, bf16[16,2,1024]{2,0,1:T(8,128)(2,1)S(1)} %all-to-all-done.2), kind=kOutput, calls=%fused_computation.5 | convolution fusion | flops 122945536 | bytes 3850240 | tf_op jit(solution)/shard_map/gcd,gcf->gdf/dot_general | solution.py:82
  49.2 1.3 %all-to-all-done = bf16[8,4,2048]{2,1,0:T(4,128)(2,1)S(1)} async-done(((bf16[8,4,2048]{2,1,0:T(4,128)(2,1)}), bf16[8,4,2048]{2,1,0:T(4,128)(2,1)S(1)}, u32[]{:S(2)}, u32[]{:S(2)}) %all-to-all-start) | async-done | bytes 131104 | tf_op jit(solution)/shard_map/all_to_all | solution.py:63
  50.5 1.1 %fusion.2 = bf16[1,128,2048]{2,1,0:T(8,128)(2,1)} fusion(bf16[32,2048]{1,0:T(8,128)(2,1)S(1)} %reshape.250, s32[32]{0:T(128)S(1)} %eq.100, pred[32]{0:T(512)(128)(4,1)S(1)} %and.91), kind=kOutput, calls=%fused_computation.7 | convolution fusion | flops 17047552 | bytes 655520 | tf_op jit(solution)/shard_map/dot_general | solution.py:74
  (21 shorter events, 0.4 us)
Async XLA Ops:
  7.2 2.6 %copy-start = (bf16[1,128,2048]{2,1,0:T(8,128)(2,1)S(1)}, bf16[1,128,2048]{2,1,0:T(8,128)(2,1)}, u32[]{:S(2)}) copy-start(bf16[1,128,2048]{2,1,0:T(8,128)(2,1)} %param.5) | copy-start | bytes 1572868
  7.2 23.4 %all-gather.2.cloned.1.call-start = ((), (), s32[]{:S(2)}) async-start(), calls=%async_computation.3 | async-start | bytes 11010048 | tf_op jit(solution)/shard_map/all_gather | solution.py:51
  11.3 14.6 %all-to-all-start.1 = ((bf16[8,4,2048]{2,1,0:T(4,128)(2,1)}), bf16[8,4,2048]{2,1,0:T(4,128)(2,1)S(1)}, u32[]{:S(2)}, u32[]{:S(2)}) async-start(bf16[8,4,2048]{2,1,0:T(4,128)(2,1)} %bitcast.10), calls=%async_computation.1 | async-start | bytes 262144 | tf_op jit(solution)/shard_map/all_to_all | solution.py:35
  27.2 10.0 %all-to-all-start.2 = ((bf16[16,2,1024]{2,0,1:T(8,128)(2,1)}), bf16[16,2,1024]{2,0,1:T(8,128)(2,1)S(1)}, u32[]{:S(2)}, u32[]{:S(2)}) async-start(bf16[16,2,1024]{2,0,1:T(8,128)(2,1)} %bitcast.67), calls=%async_computation.2 | async-start | bytes 131072 | tf_op jit(solution)/shard_map/all_to_all | solution.py:78
  37.2 13.3 %all-to-all-start = ((bf16[8,4,2048]{2,1,0:T(4,128)(2,1)}), bf16[8,4,2048]{2,1,0:T(4,128)(2,1)S(1)}, u32[]{:S(2)}, u32[]{:S(2)}) async-start(bf16[8,4,2048]{2,1,0:T(4,128)(2,1)} %broadcast_select_fusion), calls=%async_computation | async-start | bytes 262144 | tf_op jit(solution)/shard_map/all_to_all | solution.py:63
Sparse Core Ops, SparseCore 0:
  9.5 21.0 all-gather.1
where the time goes:
time: 59 us; the launch traced here: 58.4 us
  starting transfers between devices  16.4 us (28%)
  between operations  14.1 us (24%)
  matrix products  10.5 us (18%)
  waiting for transfers between devices  6.92 us (12%)
  local copies, waits for them, and re-layouts  4.56 us (8%)
  other arithmetic  4.02 us (7%)
  blocking collectives  1.88 us (3%)
    all_to_all x1, starting transfers between devices, local(): lax.all_to_all(outgoing_all.reshape(owners, MOST, features), ('expert', '...  7.28 us
    all_to_all x1, starting transfers between devices, local(): lax.all_to_all(returning, ('expert', 'tensor'), split_axis=0, concat_axis...  5.83 us
    dot_general x1, matrix products, local(): lax.dot_general(scaled, lax.all_gather(proj_weight, 'dp', axis=1, tiled=T...  5.11 us
    all_to_all x1, waiting for transfers between devices, local(): lax.all_to_all(outgoing_all.reshape(owners, MOST, features), ('expert', '...  4.91 us
    dot_general x1, matrix products, local(): jnp.einsum('gcd,gcf->gdf', column_share, scaled_all, preferred_element_ty...  4.31 us
    all_to_all x1, starting transfers between devices, local(): lax.all_to_all(slot_rows, 'dp', split_axis=1, concat_axis=0, tiled=True)  3.3 us
    all_gather x1, blocking collectives, local(): scaled_all = lax.all_gather(scaled, 'dp', axis=0, tiled=True)  1.88 us
    all_to_all x1, waiting for transfers between devices, local(): lax.all_to_all(returning, ('expert', 'tensor'), split_axis=0, concat_axis...  1.25 us
  transfers between devices with their start and end apart: 4, of which 3 were waited for; matrix products, arithmetic and copies ran while one was open for 31% of the time, Pallas kernels for 0%

commit v1 on v0

--- a/solution.py
+++ b/solution.py
@@ -32,13 +32,20 @@
     send_row = jnp.sum(jnp.where(selector, local_row[:, None, :], 0), axis=2)
     outgoing = jnp.where(filled[..., None], token_rows[send_row], jnp.zeros((), jnp.bfloat16))
     outgoing_all = jnp.broadcast_to(outgoing[:, None, None], (experts, 2, n_tensor, MOST, features))
-    incoming = lax.all_to_all(
-        outgoing_all.reshape(owners, MOST, features),
-        ("expert", "tensor"),
-        split_axis=0,
-        concat_axis=0,
-        tiled=True,
-    )
+    x = outgoing_all.reshape(owners, MOST, features)
+    ways, here = (lax.axis_size(("expert", "tensor")), lax.axis_index(("expert", "tensor")))
+    width = x.shape[0] // ways
+    shape = list(x.shape)
+    shape[0] = width
+    height = shape[0]
+    shape[0] = height * ways
+    full = jnp.zeros(shape, x.dtype)
+    for mask in range(ways):
+        part = lax.dynamic_slice_in_dim(x, (here ^ mask) * width, width, axis=0)
+        if mask:
+            part = lax.ppermute(part, ("expert", "tensor"), [(d, d ^ mask) for d in range(ways)])
+        full = lax.dynamic_update_slice_in_dim(full, part, (here ^ mask) * height, axis=0)
+    incoming = full
     incoming = incoming.reshape(owners * MOST, features)
     own_index = own_expert // 2
     own_owners = lax.dynamic_index_in_dim(owner_of, own_index, 0, keepdims=False)

time: 59 us -> 63.2 us (1.071)
  starting transfers between devices: 16.4 us -> 19.3 us
  waiting for transfers between devices: 6.92 us -> 8.51 us
    ppermute x0 -> x7, starting transfers between devices: none -> 12.6 us  [local(): lax.ppermute(part, ('expert', 'tensor'), [(d, d ^ mask) for d in range(wa...]
    all_to_all x1 -> x0, starting transfers between devices: 7.28 us -> none  [local(): lax.all_to_all(outgoing_all.reshape(owners, MOST, features), ('expert', '...]
    ppermute x0 -> x7, waiting for transfers between devices: none -> 6.29 us  [local(): lax.ppermute(part, ('expert', 'tensor'), [(d, d ^ mask) for d in range(wa...]
    all_to_all x1 -> x0, waiting for transfers between devices: 4.91 us -> none  [local(): lax.all_to_all(outgoing_all.reshape(owners, MOST, features), ('expert', '...]
    all_to_all x1, starting transfers between devices: 5.83 us -> 3.37 us  [local(): lax.all_to_all(returning, ('expert', 'tensor'), split_axis=0, concat_axis...]
    broadcast_in_dim x1, local copies, waits for them, and re-layouts: 0.69 us -> 0.04 us  [local(): jnp.broadcast_to(outgoing[:, None, None], (experts, 2, n_tensor, MOST, fe...]
  transfers between devices with their start and end apart: 4 -> 10, of which waited for: 3 -> 3; matrix products, arithmetic and copies ran while one was open for 31% -> 28% of each run, Pallas kernels for 0% -> 0%
where the time goes in v1:
time: 63.2 us; the launch traced here: 62.8 us
  starting transfers between devices  19.3 us (31%)
  between operations  14.3 us (23%)
  matrix products  10.5 us (17%)
  waiting for transfers between devices  8.51 us (13%)
  local copies, waits for them, and re-layouts  4.14 us (7%)
  other arithmetic  4.02 us (6%)
  blocking collectives  2 us (3%)
    ppermute x7, starting transfers between devices, local(): lax.ppermute(part, ('expert', 'tensor'), [(d, d ^ mask) for d in range(wa...  12.6 us
    ppermute x7, waiting for transfers between devices, local(): lax.ppermute(part, ('expert', 'tensor'), [(d, d ^ mask) for d in range(wa...  6.29 us
    dot_general x1, matrix products, local(): lax.dot_general(scaled, lax.all_gather(proj_weight, 'dp', axis=1, tiled=T...  5.11 us
    dot_general x1, matrix products, local(): jnp.einsum('gcd,gcf->gdf', column_share, scaled_all, preferred_element_ty...  4.3 us
    all_to_all x1, starting transfers between devices, local(): lax.all_to_all(returning, ('expert', 'tensor'), split_axis=0, concat_axis...  3.37 us
    all_to_all x1, starting transfers between devices, local(): lax.all_to_all(slot_rows, 'dp', split_axis=1, concat_axis=0, tiled=True)  3.3 us
    all_gather x1, blocking collectives, local(): scaled_all = lax.all_gather(scaled, 'dp', axis=0, tiled=True)  2 us
    all_to_all x1, waiting for transfers between devices, local(): lax.all_to_all(returning, ('expert', 'tensor'), split_axis=0, concat_axis...  1.52 us
  transfers between devices with their start and end apart: 10, of which 3 were waited for; matrix products, arithmetic and copies ran while one was open for 28% of the time, Pallas kernels for 0%

profile of v1, /device:TPU:0, one launch (start us, length us, event | category | flops | bytes accessed | tf_op | source)
XLA Modules:
  0.0 62.8 jit_solution(2255664588654685373)
XLA Ops:
  7.2 0.7 %all-gather.2.cloned.1.call-update = ((bf16[1,1024,1792]{2,1,0:T(8,128)(2,1)}), bf16[1,2048,1792]{2,1,0:T(8,128)(2,1)}) async-update(((), (), s32[]{:S(2)}) %all-gather.2.cloned.1.call-start, bf16[1,1024,1792]{2,1,0:T(8,128)(2,1)} %param.6) | async-update | bytes 14680088
  8.0 0.7 %broadcast_compare_fusion = (pred[2,16]{1,0:T(4,128)(4,1)S(1)}, s32[2,16]{1,0:T(2,128)S(1)}) fusion(s32[]{:T(128)S(6)} %add.112, s32[1,2,16]{2,1,0:T(2,128)} %param.9), kind=kLoop, calls=%fused_computation.68 | loop fusion | flops 512 | bytes 292 | tf_op jit(solution)/shard_map/eq | solution.py:29
  8.7 0.2 convert_reduce_fusion.1
  8.8 0.7 %and_select_fusion.1 = s32[2,16]{1,0:T(2,128)S(1)} fusion(s32[1,2,16]{2,1,0:T(2,128)} %param.9), kind=kLoop, calls=%fused_computation.59 | loop fusion | flops 352 | bytes 256 | tf_op jit(solution)/shard_map/jit(remainder)/select_n | solution.py:23
  9.5 0.1 select_reduce_fusion
  9.8 0.6 gather_fusion.1
  10.4 0.2 fusion.19
  10.6 0.1 broadcast_select_fusion.1
  10.8 3.0 %collective-permute-start = (bf16[1,4,2048]{2,1,0:T(4,128)(2,1)S(1)}, bf16[1,4,2048]{2,1,0:T(4,128)(2,1)S(1)}, u32[]{:S(2)}, u32[]{:S(2)}) collective-permute-start(bf16[1,4,2048]{2,1,0:T(4,128)(2,1)S(1)} %get-tuple-element.10), channel_id=1, source_target_pairs={{0,1},{1,0},{4,5},{5,4},{8,9},{9,8},{12,13},{13,12},{2,3},{3,2},{6... | collective-permute-start | bytes 49160 | tf_op jit(solution)/shard_map/ppermute | solution.py:46
  13.9 1.6 %collective-permute-start.1 = (bf16[1,4,2048]{2,1,0:T(4,128)(2,1)S(1)}, bf16[1,4,2048]{2,1,0:T(4,128)(2,1)S(1)}, u32[]{:S(2)}, u32[]{:S(2)}) collective-permute-start(bf16[1,4,2048]{2,1,0:T(4,128)(2,1)S(1)} %get-tuple-element.9), channel_id=1, source_target_pairs={{0,4},{1,5},{4,0},{5,1},{8,12},{9,13},{12,8},{13,9},{2,6},{3,7},{6... | collective-permute-start | bytes 49160 | tf_op jit(solution)/shard_map/ppermute | solution.py:46
  15.5 3.0 %collective-permute-start.3 = (bf16[1,4,2048]{2,1,0:T(4,128)(2,1)S(1)}, bf16[1,4,2048]{2,1,0:T(4,128)(2,1)S(1)}, u32[]{:S(2)}, u32[]{:S(2)}) collective-permute-start(bf16[1,4,2048]{2,1,0:T(4,128)(2,1)S(1)} %get-tuple-element.7), channel_id=1, source_target_pairs={{0,8},{1,9},{4,12},{5,13},{8,0},{9,1},{12,4},{13,5},{2,10},{3,11},... | collective-permute-start | bytes 49160 | tf_op jit(solution)/shard_map/ppermute | solution.py:46
  18.5 1.3 %collective-permute-start.4 = (bf16[1,4,2048]{2,1,0:T(4,128)(2,1)S(1)}, bf16[1,4,2048]{2,1,0:T(4,128)(2,1)S(1)}, u32[]{:S(2)}, u32[]{:S(2)}) collective-permute-start(bf16[1,4,2048]{2,1,0:T(4,128)(2,1)S(1)} %get-tuple-element.6), channel_id=1, source_target_pairs={{0,9},{1,8},{4,13},{5,12},{8,1},{9,0},{12,5},{13,4},{2,11},{3,10},... | collective-permute-start | bytes 49160 | tf_op jit(solution)/shard_map/ppermute | solution.py:46
  19.8 0.1 fusion.17
  20.1 0.7 %fusion.21 = f32[16]{0:T(128)S(1)} fusion(f32[1,2,16]{2,1,0:T(2,128)} %param.8, s32[]{:T(128)S(6)} %select_n.124), kind=kLoop, calls=%fused_computation.67 | loop fusion | bytes 132 | tf_op jit(solution)/shard_map/jit(dynamic_index_in_dim)/dynamic_slice | solution.py:54
  20.8 0.2 and_reduce_fusion
  21.0 0.9 %fusion.8 = bf16[16,1792]{1,0:T(8,128)(2,1)S(1)} fusion(bf16[1,1,16,1792]{3,2,1,0:T(8,128)(2,1)} %param.7, f32[16]{0:T(128)S(1)} %fusion.21), kind=kLoop, calls=%fused_computation.14 | loop fusion | flops 86016 | bytes 114752 | tf_op jit(solution)/shard_map/convert_element_type | solution.py:55
  21.9 0.1 copy.10
  22.1 0.1 and.91
  22.2 3.7 %collective-permute-start.5 = (bf16[1,4,2048]{2,1,0:T(4,128)(2,1)S(1)}, bf16[1,4,2048]{2,1,0:T(4,128)(2,1)S(1)}, u32[]{:S(2)}, u32[]{:S(2)}) collective-permute-start(bf16[1,4,2048]{2,1,0:T(4,128)(2,1)S(1)} %get-tuple-element.5), channel_id=1, source_target_pairs={{0,12},{1,13},{4,8},{5,9},{8,4},{9,5},{12,0},{13,1},{2,14},{3,15},... | collective-permute-start | bytes 49160 | tf_op jit(solution)/shard_map/ppermute | solution.py:46
  26.1 1.7 %collective-permute-done.5 = bf16[1,4,2048]{2,1,0:T(4,128)(2,1)S(1)} collective-permute-done((bf16[1,4,2048]{2,1,0:T(4,128)(2,1)S(1)}, bf16[1,4,2048]{2,1,0:T(4,128)(2,1)S(1)}, u32[]{:S(2)}, u32[]{:S(2)}) %collective-permute-start.5) | collective-permute-done | bytes 16416 | tf_op jit(solution)/shard_map/ppermute | solution.py:46
  27.8 4.6 %collective-permute-done.6 = bf16[1,4,2048]{2,1,0:T(4,128)(2,1)S(1)} collective-permute-done((bf16[1,4,2048]{2,1,0:T(4,128)(2,1)S(1)}, bf16[1,4,2048]{2,1,0:T(4,128)(2,1)S(1)}, u32[]{:S(2)}, u32[]{:S(2)}) %collective-permute-start.6) | collective-permute-done | bytes 16416 | tf_op jit(solution)/shard_map/ppermute | solution.py:46
  32.4 0.6 gather_fusion.2
  33.0 0.6 %copy.15 = bf16[2,2,8,1024]{3,2,0,1:T(8,128)(2,1)} copy(bf16[2,2,8,1024]{3,2,1,0:T(8,128)(2,1)S(1)} %bitcast.72) | data formatting | bytes 131072 | tf_op jit(solution)/shard_map/all_to_all | solution.py:85
  33.7 3.3 %all-to-all-start.1 = ((bf16[16,2,1024]{2,0,1:T(8,128)(2,1)}), bf16[16,2,1024]{2,0,1:T(8,128)(2,1)S(1)}, u32[]{:S(2)}, u32[]{:S(2)}) async-start(bf16[16,2,1024]{2,0,1:T(8,128)(2,1)} %bitcast.67), calls=%async_computation.1 | async-start | bytes 131072 | tf_op jit(solution)/shard_map/all_to_all | solution.py:85
  37.0 5.1 %fusion.3 = bf16[16,2048]{1,0:T(8,128)(2,1)S(1)} fusion(bf16[1,2048,1792]{2,1,0:T(8,128)(2,1)} %all-gather.2.cloned.1.call-done, bf16[1,1,16,1792]{3,2,1,0:T(8,128)(2,1)} %param.7, f32[16]{0:T(128)S(1)} %fusion.21), kind=kOutput, calls=%fused_computation.8 | convolution fusion | flops 117559296 | bytes 7462976 | tf_op jit(solution)/shard_map/dot_general | solution.py:56
  42.1 0.7 %gather_fusion = bf16[32,2048]{1,0:T(8,128)(2,1)S(1)} fusion(bf16[16,2048]{1,0:T(8,128)(2,1)S(1)} %fusion.3, s32[1024]{0:T(1024)S(1)} %pad_clamp_fusion.2), kind=kCustom, calls=%fused_computation | custom fusion | bytes 262272 | tf_op jit(solution)/shard_map/gather | solution.py:68
  42.8 0.8 %broadcast_select_fusion = bf16[8,4,2048]{2,1,0:T(4,128)(2,1)} fusion(bf16[8,4,2048]{2,1,0:T(4,128)(2,1)S(1)} %reshape.256, pred[8,4]{1,0:T(8,128)(4,1)S(1)} %copy.10), kind=kLoop, calls=%fused_computation.11 | loop fusion | flops 65536 | bytes 262176 | tf_op jit(solution)/shard_map/jit(_where)/select_n | solution.py:67
  43.6 3.4 %all-to-all-start = ((bf16[8,4,2048]{2,1,0:T(4,128)(2,1)}), bf16[8,4,2048]{2,1,0:T(4,128)(2,1)S(1)}, u32[]{:S(2)}, u32[]{:S(2)}) async-start(bf16[8,4,2048]{2,1,0:T(4,128)(2,1)} %broadcast_select_fusion), calls=%async_computation | async-start | bytes 262144 | tf_op jit(solution)/shard_map/all_to_all | solution.py:70
  47.0 2.0 %all_gather.7 = bf16[32,1792]{1,0:T(8,128)(2,1)S(1)} all-gather(bf16[16,1792]{1,0:T(8,128)(2,1)S(1)} %fusion.8), channel_id=1, replica_groups=mesh['groups'=2,'expert'=4,'dp'=2,'tensor'=2] {'dp'}, dimensions={0}, use_global_device_ids=true | all-gather | bytes 172032 | tf_op jit(solution)/shard_map/all_gather | solution.py:86
  49.0 4.3 %convert_reduce_fusion = bf16[1024,1792]{1,0:T(8,128)(2,1)} fusion(bf16[2,16,1792]{2,1,0:T(8,128)(2,1)S(1)} %bitcast.71, bf16[16,2,1024]{2,0,1:T(8,128)(2,1)S(1)} %all-to-all-done.1), kind=kOutput, calls=%fused_computation.5 | convolution fusion | flops 122945536 | bytes 3850240 | tf_op jit(solution)/shard_map/gcd,gcf->gdf/dot_general | solution.py:89
  53.3 1.5 %all-to-all-done = bf16[8,4,2048]{2,1,0:T(4,128)(2,1)S(1)} async-done(((bf16[8,4,2048]{2,1,0:T(4,128)(2,1)}), bf16[8,4,2048]{2,1,0:T(4,128)(2,1)S(1)}, u32[]{:S(2)}, u32[]{:S(2)}) %all-to-all-start) | async-done | bytes 131104 | tf_op jit(solution)/shard_map/all_to_all | solution.py:70
  54.9 1.1 %fusion.2 = bf16[1,128,2048]{2,1,0:T(8,128)(2,1)} fusion(bf16[32,2048]{1,0:T(8,128)(2,1)S(1)} %reshape.250, s32[32]{0:T(128)S(1)} %eq.100, pred[32]{0:T(512)(128)(4,1)S(1)} %and.91), kind=kOutput, calls=%fused_computation.7 | convolution fusion | flops 17047552 | bytes 655520 | tf_op jit(solution)/shard_map/dot_general | solution.py:81
  (42 shorter events, 1.0 us)
Async XLA Ops:
  7.2 2.6 %copy-start = (bf16[1,128,2048]{2,1,0:T(8,128)(2,1)S(1)}, bf16[1,128,2048]{2,1,0:T(8,128)(2,1)}, u32[]{:S(2)}) copy-start(bf16[1,128,2048]{2,1,0:T(8,128)(2,1)} %param.5) | copy-start | bytes 1572868
  7.2 29.8 %all-gather.2.cloned.1.call-start = ((), (), s32[]{:S(2)}) async-start(), calls=%async_computation.2 | async-start | bytes 11010048 | tf_op jit(solution)/shard_map/all_gather | solution.py:58
  10.8 11.3 %collective-permute-start = (bf16[1,4,2048]{2,1,0:T(4,128)(2,1)S(1)}, bf16[1,4,2048]{2,1,0:T(4,128)(2,1)S(1)}, u32[]{:S(2)}, u32[]{:S(2)}) collective-permute-start(bf16[1,4,2048]{2,1,0:T(4,128)(2,1)S(1)} %get-tuple-element.10), channel_id=1, source_target_pairs={{0,1},{1,0},{4,5},{5,4},{8,9},{9,8},{12,13},{13,12},{2,3},{3,2},{6... | collective-permute-start | bytes 49160 | tf_op jit(solution)/shard_map/ppermute | solution.py:46
  13.9 12.0 %collective-permute-start.1 = (bf16[1,4,2048]{2,1,0:T(4,128)(2,1)S(1)}, bf16[1,4,2048]{2,1,0:T(4,128)(2,1)S(1)}, u32[]{:S(2)}, u32[]{:S(2)}) collective-permute-start(bf16[1,4,2048]{2,1,0:T(4,128)(2,1)S(1)} %get-tuple-element.9), channel_id=1, source_target_pairs={{0,4},{1,5},{4,0},{5,1},{8,12},{9,13},{12,8},{13,9},{2,6},{3,7},{6... | collective-permute-start | bytes 49160 | tf_op jit(solution)/shard_map/ppermute | solution.py:46
  15.5 10.5 %collective-permute-start.2 = (bf16[1,4,2048]{2,1,0:T(4,128)(2,1)S(1)}, bf16[1,4,2048]{2,1,0:T(4,128)(2,1)S(1)}, u32[]{:S(2)}, u32[]{:S(2)}) collective-permute-start(bf16[1,4,2048]{2,1,0:T(4,128)(2,1)S(1)} %get-tuple-element.8), channel_id=1, source_target_pairs={{0,5},{1,4},{4,1},{5,0},{8,13},{9,12},{12,9},{13,8},{2,7},{3,6},{6... | collective-permute-start | bytes 49160 | tf_op jit(solution)/shard_map/ppermute | solution.py:46
  15.5 10.5 %collective-permute-start.3 = (bf16[1,4,2048]{2,1,0:T(4,128)(2,1)S(1)}, bf16[1,4,2048]{2,1,0:T(4,128)(2,1)S(1)}, u32[]{:S(2)}, u32[]{:S(2)}) collective-permute-start(bf16[1,4,2048]{2,1,0:T(4,128)(2,1)S(1)} %get-tuple-element.7), channel_id=1, source_target_pairs={{0,8},{1,9},{4,12},{5,13},{8,0},{9,1},{12,4},{13,5},{2,10},{3,11},... | collective-permute-start | bytes 49160 | tf_op jit(solution)/shard_map/ppermute | solution.py:46
  18.5 7.6 %collective-permute-start.4 = (bf16[1,4,2048]{2,1,0:T(4,128)(2,1)S(1)}, bf16[1,4,2048]{2,1,0:T(4,128)(2,1)S(1)}, u32[]{:S(2)}, u32[]{:S(2)}) collective-permute-start(bf16[1,4,2048]{2,1,0:T(4,128)(2,1)S(1)} %get-tuple-element.6), channel_id=1, source_target_pairs={{0,9},{1,8},{4,13},{5,12},{8,1},{9,0},{12,5},{13,4},{2,11},{3,10},... | collective-permute-start | bytes 49160 | tf_op jit(solution)/shard_map/ppermute | solution.py:46
  22.2 5.6 %collective-permute-start.5 = (bf16[1,4,2048]{2,1,0:T(4,128)(2,1)S(1)}, bf16[1,4,2048]{2,1,0:T(4,128)(2,1)S(1)}, u32[]{:S(2)}, u32[]{:S(2)}) collective-permute-start(bf16[1,4,2048]{2,1,0:T(4,128)(2,1)S(1)} %get-tuple-element.5), channel_id=1, source_target_pairs={{0,12},{1,13},{4,8},{5,9},{8,4},{9,5},{12,0},{13,1},{2,14},{3,15},... | collective-permute-start | bytes 49160 | tf_op jit(solution)/shard_map/ppermute | solution.py:46
  25.9 6.5 %collective-permute-start.6 = (bf16[1,4,2048]{2,1,0:T(4,128)(2,1)S(1)}, bf16[1,4,2048]{2,1,0:T(4,128)(2,1)S(1)}, u32[]{:S(2)}, u32[]{:S(2)}) collective-permute-start(bf16[1,4,2048]{2,1,0:T(4,128)(2,1)S(1)} %get-tuple-element.4), channel_id=1, source_target_pairs={{0,13},{1,12},{4,9},{5,8},{8,5},{9,4},{12,1},{13,0},{2,15},{3,14},... | collective-permute-start | bytes 49160 | tf_op jit(solution)/shard_map/ppermute | solution.py:46
  33.7 10.0 %all-to-all-start.1 = ((bf16[16,2,1024]{2,0,1:T(8,128)(2,1)}), bf16[16,2,1024]{2,0,1:T(8,128)(2,1)S(1)}, u32[]{:S(2)}, u32[]{:S(2)}) async-start(bf16[16,2,1024]{2,0,1:T(8,128)(2,1)} %bitcast.67), calls=%async_computation.1 | async-start | bytes 131072 | tf_op jit(solution)/shard_map/all_to_all | solution.py:85
  43.6 11.2 %all-to-all-start = ((bf16[8,4,2048]{2,1,0:T(4,128)(2,1)}), bf16[8,4,2048]{2,1,0:T(4,128)(2,1)S(1)}, u32[]{:S(2)}, u32[]{:S(2)}) async-start(bf16[8,4,2048]{2,1,0:T(4,128)(2,1)} %broadcast_select_fusion), calls=%async_computation | async-start | bytes 262144 | tf_op jit(solution)/shard_map/all_to_all | solution.py:70
Sparse Core Ops, SparseCore 0:
  9.5 21.0 all-gather.1
